TPU v7x, 32 devices: a 4x4x1 block of a 4x4x8 slice. The times are simulated.
32 devices in a mesh: dp: 1 (over z), eo: 4 (over y), em: 4 (over x), ei: 2 (over core).
Axes of the slice: x: 4, y: 4, z: 1, core: 2. Of those that a mesh axis runs over, the one named last changes fastest.
The devices are a block of a 4x4x8 slice.
Arguments:
- x_disp: bfloat16 [32, 64, 24, 2048], P('dp', ('eo', 'em', 'ei'))
- w_gate: bfloat16 [64, 2048, 1408], P(('eo', 'em', 'ei'))
- w_up: bfloat16 [64, 2048, 1408], P(('eo', 'em', 'ei'))
- w_down: bfloat16 [64, 1408, 2048], P(('eo', 'em', 'ei'))
- slot_idx: int32 [4096, 6], P(('dp', 'eo', 'em', 'ei'))
- expert_idx: int32 [4096, 6], P(('dp', 'eo', 'em', 'ei'))
- gate_wt: float32 [4096, 6], P(('dp', 'eo', 'em', 'ei'))
Outputs:
- output: bfloat16 [4096, 2048], P(('dp', 'eo', 'em', 'ei'))
All inputs are finite; a program needn't handle non-finite values.
Results may differ from a plain program's by a relative error of at most 0.00133.
Values are sent between devices in bfloat16 or wider.
A program may use at most 768 MiB of HBM per device.

v0:
```python
import jax
import jax.numpy as jnp
from jax import lax
from jax.sharding import PartitionSpec as P

GROUP_AXES = ('eo', 'em', 'ei')


def combine_rows(flat_rows, slot_idx, expert_idx, gate_wt, slot_count):
    is_live = slot_idx >= 0
    row_index = jnp.where(is_live, expert_idx * slot_count + slot_idx, 0)
    weight = jnp.where(is_live, gate_wt, 0.0)
    picked = jnp.take(flat_rows, row_index, axis=0)
    combined = jnp.sum(weight[:, :, None] * picked.astype(jnp.float32), axis=1)
    return combined.astype(jnp.bfloat16)


def solution(mesh):
    token_spec = P(('dp',) + GROUP_AXES, None)
    weight_spec = P(GROUP_AXES, None, None)
    rows_spec = P('dp', GROUP_AXES, None, None)

    def local_part(x_local, w_gate, w_up, w_down, slot_idx, expert_idx, gate_wt):
        slot_count = x_local.shape[2]
        model_width = x_local.shape[3]
        gate_pre = jnp.einsum('secd,edf->escf', x_local, w_gate, preferred_element_type=jnp.float32)
        up_pre = jnp.einsum('secd,edf->escf', x_local, w_up, preferred_element_type=jnp.float32)
        hidden = (jax.nn.silu(gate_pre) * up_pre).astype(jnp.bfloat16)
        y_rows = jnp.einsum('escf,efd->escd', hidden, w_down, preferred_element_type=jnp.float32).astype(jnp.bfloat16)
        returned = lax.all_to_all(y_rows, GROUP_AXES, 1, 0, tiled=True)
        flat_rows = returned.reshape(-1, model_width)
        return combine_rows(flat_rows, slot_idx, expert_idx, gate_wt, slot_count)

    return jax.shard_map(local_part, mesh=mesh,
                         in_specs=(rows_spec, weight_spec, weight_spec, weight_spec, token_spec, token_spec, token_spec),
                         out_specs=token_spec, check_vma=False)
```

profile of v0, /device:TPU:103, one launch (start us, length us, event | category | flops | bytes accessed | tf_op | source)
XLA Modules:
  0.0 163.1 jit_solution(9590172289823755184)
XLA Ops:
  0.0 0.0 slice-start
  0.0 0.0 slice-start.1
  0.0 16.9 %fusion.2 = f32[2,32,24,1408]{3,2,1,0:T(8,128)} fusion(bf16[2,2048,1408]{2,1,0:T(8,128)(2,1)} %param.9, bf16[32,2,24,2048]{3,2,1,0:T(8,128)(2,1)} %param.7), kind=kOutput, calls=%fused_computation.3 | convolution fusion | flops 8858370048 | bytes 26476544 | tf_op jit(solution)/shard_map/secd,edf->escf/dot_general | solution.py:27
  17.0 0.0 slice-start.2
  17.0 18.9 %multiply_convert_fusion = bf16[2,32,24,1408]{3,2,1,0:T(8,128)(2,1)} fusion(f32[2,32,24,1408]{3,2,1,0:T(8,128)} %fusion.2, bf16[2,2048,1408]{2,1,0:T(8,128)(2,1)} %param.8, bf16[32,2,24,2048]{3,2,1,0:T(8,128)(2,1)} %param.7), kind=kOutput, calls=%fused_computation.7 | convolution fusion | flops 8871346176 | bytes 30801920 | tf_op jit(solution)/shard_map/secd,edf->escf/dot_general | solution.py:26
  35.9 0.0 slice-done
  35.9 0.0 slice-done.1
  35.9 0.0 slice-done.2
  35.9 12.0 %fusion.10 = bf16[2,32,24,2048]{3,2,1,0:T(8,128)(2,1)S(1)} fusion(bf16[2,32,24,1408]{3,2,1,0:T(8,128)(2,1)} %multiply_convert_fusion, bf16[2,1408,2048]{2,1,0:T(8,128)(2,1)S(1)} %bitcast.26), kind=kOutput, calls=%fused_computation.11 | convolution fusion | flops 8861515776 | bytes 22151168 | tf_op jit(solution)/shard_map/escf,efd->escd/dot_general | solution.py:29
  47.9 3.2 %copy.20 = bf16[2,32,24,2048]{3,2,0,1:T(8,128)(2,1)} copy(bf16[2,32,24,2048]{3,2,1,0:T(8,128)(2,1)S(1)} %fusion.10) | data formatting | bytes 12582912 | tf_op jit(solution)/shard_map/convert_element_type | solution.py:29
  51.1 0.0 copy-start
  51.1 0.0 copy-start.2
  51.1 0.0 copy-start.1
  51.1 8.0 %all-to-all-start = ((bf16[2,32,24,2048]{3,2,0,1:T(8,128)(2,1)}), bf16[2,32,24,2048]{3,2,0,1:T(8,128)(2,1)}, u32[]{:S(2)}, u32[]{:S(2)}) async-start(bf16[2,32,24,2048]{3,2,0,1:T(8,128)(2,1)} %copy.20), calls=%async_computation | async-start | bytes 12582912 | tf_op jit(solution)/shard_map/all_to_all | solution.py:30
  59.1 0.0 copy-done
  59.1 0.0 copy-done.2
  59.2 0.1 copy.21
  59.3 0.1 reshape.13
  59.4 0.0 copy-done.1
  59.4 0.1 copy.16
  59.6 0.1 copy.17
  59.7 83.8 %all-to-all-done = bf16[2,32,24,2048]{3,2,0,1:T(8,128)(2,1)} async-done(((bf16[2,32,24,2048]{3,2,0,1:T(8,128)(2,1)}), bf16[2,32,24,2048]{3,2,0,1:T(8,128)(2,1)}, u32[]{:S(2)}, u32[]{:S(2)}) %all-to-all-start) | async-done | bytes 6291488 | tf_op jit(solution)/shard_map/all_to_all | solution.py:30
  143.5 9.9 %gather_fusion = bf16[768,2048]{1,0:T(8,128)(2,1)S(1)} fusion(bf16[1536,2048]{1,0:T(8,128)(2,1)} %bitcast.8, s32[1024]{0:T(1024)S(1)} %pad_clamp_fusion), kind=kCustom, calls=%fused_computation | custom fusion | bytes 6294528 | tf_op jit(solution)/shard_map/jit(_take)/gather | solution.py:13
  153.5 2.9 %reshape.12 = bf16[128,6,2048]{2,1,0:T(8,128)(2,1)} reshape(bf16[768,2048]{1,0:T(8,128)(2,1)S(1)} %gather_fusion) | data formatting | bytes 6291456 | tf_op jit(solution)/shard_map/jit(_take)/gather | solution.py:13
  156.3 6.8 %multiply_reduce_fusion = bf16[128,2048]{1,0:T(8,128)(2,1)} fusion(bf16[128,6,2048]{2,1,0:T(8,128)(2,1)} %reshape.12, f32[128,6]{1,0:T(8,128)S(1)} %copy.16, pred[128,6]{1,0:T(8,128)(4,1)S(1)} %copy.17), kind=kLoop, calls=%fused_computation.8 | loop fusion | flops 6029312 | bytes 3673856 | tf_op jit(solution)/shard_map/reduce_sum | solution.py:14
  (4 shorter events, 0.0 us)
Async XLA Ops:
  0.0 35.9 %slice-start = ((s8[11534336]{0:T(1024)(128)(4,1)}), s8[3145728]{0:T(1024)(128)(4,1)S(1)}, s32[]{:S(2)}) async-start(s8[11534336]{0:T(1024)(128)(4,1)} %bitcast.25), calls=%async_computation.1 | async-start | bytes 6291456
  0.0 35.9 %slice-start.1 = ((s8[11534336]{0:T(1024)(128)(4,1)}), s8[4194304]{0:T(1024)(128)(4,1)S(1)}, s32[]{:S(2)}) async-start(s8[11534336]{0:T(1024)(128)(4,1)} %bitcast.25), calls=%async_computation.2 | async-start | bytes 8388608
  17.0 18.9 %slice-start.2 = ((s8[11534336]{0:T(1024)(128)(4,1)}), s8[4194304]{0:T(1024)(128)(4,1)S(1)}, s32[]{:S(2)}) async-start(s8[11534336]{0:T(1024)(128)(4,1)} %bitcast.25), calls=%async_computation.3 | async-start | bytes 8388608
  51.1 8.0 %copy-start = (s32[128,6]{0,1:T(8,128)S(1)}, s32[128,6]{0,1:T(8,128)}, u32[]{:S(2)}) copy-start(s32[128,6]{0,1:T(8,128)} %param.11) | copy-start | bytes 9220
  51.1 8.0 %copy-start.2 = (s32[128,6]{0,1:T(8,128)S(1)}, s32[128,6]{0,1:T(8,128)}, u32[]{:S(2)}) copy-start(s32[128,6]{0,1:T(8,128)} %param.12) | copy-start | bytes 9220
  51.1 8.3 %copy-start.1 = (f32[128,6]{0,1:T(8,128)S(1)}, f32[128,6]{0,1:T(8,128)}, u32[]{:S(2)}) copy-start(f32[128,6]{0,1:T(8,128)} %param.13) | copy-start | bytes 9220
  51.1 92.4 %all-to-all-start = ((bf16[2,32,24,2048]{3,2,0,1:T(8,128)(2,1)}), bf16[2,32,24,2048]{3,2,0,1:T(8,128)(2,1)}, u32[]{:S(2)}, u32[]{:S(2)}) async-start(bf16[2,32,24,2048]{3,2,0,1:T(8,128)(2,1)} %copy.20), calls=%async_computation | async-start | bytes 12582912 | tf_op jit(solution)/shard_map/all_to_all | solution.py:30
where the time goes:
time: 163 us
  waiting for transfers between devices  83.8 us (51%)
  matrix products  47.9 us (29%)
  local copies, waits for them, and re-layouts  16.5 us (10%)
  starting transfers between devices  7.98 us (5%)
  other arithmetic  6.81 us (4%)
    all_to_all x1, waiting for transfers between devices, local_part(): returned = lax.all_to_all(y_rows, GROUP_AXES, 1, 0, tiled=True)  83.8 us
    dot_general x1, matrix products, local_part(): jnp.einsum('secd,edf->escf', x_local, w_gate, preferred_element_type=jnp....  18.9 us
    dot_general x1, matrix products, local_part(): jnp.einsum('secd,edf->escf', x_local, w_up, preferred_element_type=jnp.fl...  16.9 us
    gather x2, local copies, waits for them, and re-layouts, combine_rows(): picked = jnp.take(flat_rows, row_index, axis=0)  12.8 us
    dot_general x1, matrix products, local_part(): jnp.einsum('escf,efd->escd', hidden, w_down, preferred_element_type=jnp.f...  12 us
    all_to_all x1, starting transfers between devices, local_part(): returned = lax.all_to_all(y_rows, GROUP_AXES, 1, 0, tiled=True)  7.98 us
    reduce_sum x1, other arithmetic, combine_rows(): combined = jnp.sum(weight[:, :, None] * picked.astype(jnp.float32), axis=1)  6.79 us
  transfers between devices with their start and end apart: 1, of which 1 were waited for; matrix products, arithmetic and copies ran while one was open for 0% of the time, Pallas kernels for 0%

commit v1 on v0

v1 whole, which is shorter than its diff:
```python
import functools

import jax
import jax.numpy as jnp
from jax import lax
from jax.experimental import pallas as pl
from jax.experimental.pallas import tpu as pltpu
from jax.sharding import PartitionSpec as P

GROUP_AXES = ('eo', 'em', 'ei')
MESH = pl.DeviceIdType.MESH
TILE = 256
ROUTE_ROWS = 8


def kernel(n, cores, slots, top, x_hbm, wg_hbm, wu_hbm, wd_hbm, route_ref, out_ref,
           wg, wu, wl, wd, xs, xe, hid, ybuf, recv, part, prec, own, routes,
           gu_sem, wl_sem, wd_sem, x_sem, s1, r1, s2, r2, s3, r3):
    experts, model, ff = wg_hbm.shape
    ff_main = wg.shape[2]
    half = ff - ff_main
    rows = experts * slots
    tokens = out_ref.shape[0]
    y, x, c = (lax.axis_index(a) for a in GROUP_AXES)

    def wrap(v):
        return lax.rem(v, n)

    barrier = pltpu.get_barrier_semaphore()
    for oy in range(n):
        for ox in range(n):
            for oc in range(cores):
                if oy or ox or oc:
                    pl.semaphore_signal(barrier, inc=1, device_id_type=MESH, device_id={
                        'eo': wrap(y + oy), 'em': wrap(x + ox), 'ei': lax.rem(c + oc, cores)})

    def x_copies(i):
        step = wrap(i + 1)
        buf = lax.rem(i, 2)
        out = []
        for t in range(2):
            for j in range(n):
                if t == 0:
                    src = (wrap(y + step) * n + wrap(x + j)) * cores
                else:
                    src = (wrap(y + j) * n + wrap(x + step)) * cores + 1
                d = t * n + j
                out.append(pltpu.make_async_copy(x_hbm.at[src], xs.at[buf, d], x_sem.at[buf, d]))
        return out

    main_tiles = ff_main // TILE

    def gate_up_copies(e, k):
        if k < main_tiles:
            cols = pl.ds(k * TILE, TILE)
            return [pltpu.make_async_copy(w.at[e, :, cols], v.at[e, :, cols], gu_sem.at[e, k, a])
                    for a, (w, v) in enumerate(((wg_hbm, wg), (wu_hbm, wu)))]
        cols = pl.ds(ff_main, half)
        return [pltpu.make_async_copy(w.at[e, :, cols], wl.at[e, :, pl.ds(a * half, half)], wl_sem.at[e, a])
                for a, w in enumerate((wg_hbm, wu_hbm))]

    def down_copies(e, k):
        cols = pl.ds(k * TILE, TILE)
        return [pltpu.make_async_copy(wd_hbm.at[e, :, cols], wd.at[e, :, cols], wd_sem.at[e, k])]

    down_tiles = model // TILE
    for cp in x_copies(0):
        cp.start()
    for e in range(experts):
        for k in range(main_tiles + 1):
            for cp in gate_up_copies(e, k):
                cp.start()
    for k in range(down_tiles):
        for e in range(experts):
            for cp in down_copies(e, k):
                cp.start()

    def compute(i, first):
        buf = lax.rem(i, 2)
        for cp in x_copies(i):
            cp.wait()
        for k in range(0, model, 2 * TILE):
            cols = pl.ds(k, 2 * TILE)
            pieces = [xs[buf, d, :, cols].astype(jnp.float32) for d in range(2 * n)]
            for e in range(experts):
                xe[e, :, cols] = jnp.concatenate(
                    [p[e * slots:(e + 1) * slots] for p in pieces], axis=0).astype(jnp.bfloat16)
        for e in range(experts):
            for k in range(main_tiles + 1):
                if first:
                    for cp in gate_up_copies(e, k):
                        cp.wait()
                if k < main_tiles:
                    cols = pl.ds(k * TILE, TILE)
                    g = jnp.dot(xe[e], wg[e, :, cols], preferred_element_type=jnp.float32)
                    u = jnp.dot(xe[e], wu[e, :, cols], preferred_element_type=jnp.float32)
                    hid[e, :, cols] = (jax.nn.silu(g) * u).astype(jnp.bfloat16)
                else:
                    gu = jnp.dot(xe[e], wl[e], preferred_element_type=jnp.float32)
                    hid[e, :, pl.ds(ff_main, half)] = (
                        jax.nn.silu(gu[:, :half]) * gu[:, half:]).astype(jnp.bfloat16)
        for k in range(down_tiles):
            cols = pl.ds(k * TILE, TILE)
            if first:
                for e in range(experts):
                    for cp in down_copies(e, k):
                        cp.wait()
            ys = [jnp.dot(hid[e], wd[e, :, cols], preferred_element_type=jnp.float32) for e in range(experts)]
            for d in range(2 * n):
                block = jnp.concatenate([v[d * slots:(d + 1) * slots] for v in ys], axis=0)
                ybuf[i, d // n, d % n, :, cols] = block.astype(jnp.bfloat16)

    ring = jnp.where(c == 0, x, y)

    def row_sends(i):
        out = []
        for j in range(1, n):
            out.append(pltpu.make_async_remote_copy(
                src_ref=ybuf.at[i, 0, j], dst_ref=recv.at[i, x, c], send_sem=s1.at[i, 0, j],
                recv_sem=r1.at[i, x, c], device_id={'eo': y, 'em': wrap(x + j), 'ei': 0}, device_id_type=MESH))
            out.append(pltpu.make_async_remote_copy(
                src_ref=ybuf.at[i, 1, j], dst_ref=recv.at[i, y, c], send_sem=s1.at[i, 1, j],
                recv_sem=r1.at[i, y, c], device_id={'eo': wrap(y + j), 'em': x, 'ei': 1}, device_id_type=MESH))
        other = 1 - c
        q = jnp.where(c == 0, y, x)
        out.append(pltpu.make_async_remote_copy(
            src_ref=ybuf.at[i, other, 0], dst_ref=recv.at[i, q, c], send_sem=s1.at[i, other, 0],
            recv_sem=r1.at[i, q, c], device_id={'eo': y, 'em': x, 'ei': other}, device_id_type=MESH))
        return out

    def wait_rows(i):
        def one(q, cc):
            pltpu.make_async_remote_copy(
                src_ref=ybuf.at[i, 0, 0], dst_ref=recv.at[i, q, cc], send_sem=s1.at[i, 0, 0],
                recv_sem=r1.at[i, q, cc], device_id={'eo': y, 'em': x, 'ei': 1 - c},
                device_id_type=MESH).wait_recv()
        one(ring, 1 - c)
        for j in range(1, n):
            for cc in range(cores):
                one(wrap(ring + j), cc)

    def send_rows(i):
        for cp in row_sends(i):
            cp.start()
        recv[i, ring, c] = ybuf[i, c, 0]

    along_y = jnp.where(c == 0, 1, 0)

    def ahead(step):
        return {'eo': wrap(y + step * along_y), 'em': wrap(x + step * (1 - along_y)), 'ei': c}

    def part_send(i):
        return pltpu.make_async_remote_copy(
            src_ref=part.at[i], dst_ref=prec.at[i], send_sem=s2.at[i], recv_sem=r2.at[i],
            device_id=ahead(i + 1), device_id_type=MESH)

    def route_send(i):
        return pltpu.make_async_remote_copy(
            src_ref=route_ref, dst_ref=routes.at[i], send_sem=s3.at[i], recv_sem=r3.at[i],
            device_id=ahead(n - 1 - i), device_id_type=MESH)

    def combine(i, route, store):
        taken = n * cores * rows
        r = lax.broadcasted_iota(jnp.int32, (taken, tokens), 0)
        q = sum((r >= m * cores * rows).astype(jnp.int32) for m in range(1, n))
        chip = cores * experts
        base = jnp.where(c == 0, y * (n * chip), x * chip) * slots
        jump = jnp.where(c == 0, 0, (n - 1) * chip * slots)
        key = (base + r + q * jump).astype(jnp.float32)
        weight = jnp.zeros((taken, tokens), jnp.float32)
        for j in range(top):
            weight = weight + jnp.where(route[j:j + 1, :] == key, route[ROUTE_ROWS + j:ROUTE_ROWS + j + 1, :], 0.0)
        live = jnp.max(weight, axis=1, keepdims=True) > 0
        hi = weight.astype(jnp.bfloat16)
        rest = weight - hi.astype(jnp.float32)
        mid = rest.astype(jnp.bfloat16)
        low = (rest - mid.astype(jnp.float32)).astype(jnp.bfloat16)
        lhs = jnp.concatenate([hi, mid, low], axis=1)
        for k in range(down_tiles):
            cols = pl.ds(k * TILE, TILE)
            got = recv[i, :, :, :, cols].reshape(taken, TILE)
            got = jnp.where(live, got.astype(jnp.float32), 0.0).astype(jnp.bfloat16)
            p = lax.dot_general(lhs, got, (((0,), (0,)), ((), ())), preferred_element_type=jnp.float32)
            store(cols, (p[2 * tokens:] + p[tokens:2 * tokens]) + p[:tokens])

    compute(0, True)
    for cp in x_copies(1):
        cp.start()
    pl.semaphore_wait(barrier, n * n * cores - 1)
    send_rows(0)
    for i in range(n - 1):
        route_send(i).start()
    for i in range(n - 1):
        route_send(i).wait_recv()

    @pl.loop(1, n)
    def _(i):
        compute(i, False)
        send_rows(i)

        @pl.when(i < n - 1)
        def _():
            for cp in x_copies(i + 1):
                cp.start()

        prev = i - 1
        wait_rows(prev)

        def store(cols, value):
            part[prev, :, cols] = value

        combine(prev, routes[prev], store)
        part_send(prev).start()

    wait_rows(n - 1)

    def store(cols, value):
        own[:, cols] = value

    combine(n - 1, route_ref[...], store)
    for i in range(n - 1):
        part_send(i).wait_recv()
    for k in range(down_tiles):
        cols = pl.ds(k * TILE, TILE)
        total = own[:, cols]
        for i in range(n - 1):
            total = total + prec[i, :, cols]
        out_ref[:, cols] = total.astype(out_ref.dtype)
    for i in range(n - 1):
        part_send(i).wait_send()
        route_send(i).wait_send()

    @pl.loop(0, n)
    def _(i):
        for cp in row_sends(i):
            cp.wait_send()


def solution(mesh):
    token_spec = P(('dp',) + GROUP_AXES, None)
    weight_spec = P(GROUP_AXES, None, None)
    rows_spec = P('dp', GROUP_AXES, None, None)
    n, cores = mesh.shape['eo'], mesh.shape['ei']
    assert mesh.shape['em'] == n and cores == 2

    def local_part(x_local, w_gate, w_up, w_down, slot_idx, expert_idx, gate_wt):
        sources, experts, slots, model = x_local.shape
        ff = w_gate.shape[2]
        tokens, top = slot_idx.shape
        ff_main = ff // TILE * TILE
        half = ff - ff_main
        assert 2 * half == TILE
        key = jnp.where(slot_idx >= 0, expert_idx * slots + slot_idx, -1).astype(jnp.float32)
        pad = ((0, ROUTE_ROWS - top), (0, 0))
        route = jnp.concatenate([jnp.pad(key.T, pad, constant_values=-1.0), jnp.pad(gate_wt.T, pad)], axis=0)
        rows = experts * slots
        chunk = 2 * n
        hbm = pl.BlockSpec(memory_space=pl.ANY)
        vmem = pl.BlockSpec(memory_space=pltpu.VMEM)
        dma = pltpu.SemaphoreType.DMA
        return pl.pallas_call(
            functools.partial(kernel, n, cores, slots, top),
            out_shape=jax.ShapeDtypeStruct((tokens, model), jnp.bfloat16),
            in_specs=[hbm, hbm, hbm, hbm, vmem],
            out_specs=vmem,
            scratch_shapes=[
                pltpu.VMEM((experts, model, ff_main), jnp.bfloat16),
                pltpu.VMEM((experts, model, ff_main), jnp.bfloat16),
                pltpu.VMEM((experts, model, 2 * half), jnp.bfloat16),
                pltpu.VMEM((experts, ff, model), jnp.bfloat16),
                pltpu.VMEM((2, chunk, rows, model), jnp.bfloat16),
                pltpu.VMEM((experts, chunk * slots, model), jnp.bfloat16),
                pltpu.VMEM((experts, chunk * slots, ff), jnp.bfloat16),
                pltpu.VMEM((n, 2, n, rows, model), jnp.bfloat16),
                pltpu.VMEM((n, n, cores, rows, model), jnp.bfloat16),
                pltpu.VMEM((n - 1, tokens, model), jnp.float32),
                pltpu.VMEM((n - 1, tokens, model), jnp.float32),
                pltpu.VMEM((tokens, model), jnp.float32),
                pltpu.VMEM((n - 1, 2 * ROUTE_ROWS, tokens), jnp.float32),
                dma((experts, ff_main // TILE, 2)), dma((experts, 2)), dma((experts, model // TILE)), dma((2, chunk)),
                dma((n, 2, n)), dma((n, n, cores)), dma((n - 1,)), dma((n - 1,)), dma((n - 1,)), dma((n - 1,)),
            ],
            compiler_params=pltpu.CompilerParams(
                collective_id=0, has_side_effects=True, vmem_limit_bytes=67_000_000),
        )(x_local.reshape(sources, rows, model), w_gate, w_up, w_down, route)

    return jax.shard_map(local_part, mesh=mesh,
                         in_specs=(rows_spec, weight_spec, weight_spec, weight_spec, token_spec, token_spec, token_spec),
                         out_specs=token_spec, check_vma=False)
```

time: 163 us -> 111 us (0.68)
  the two profiles are of different devices: /device:TPU:103 before, /device:TPU:99 now
where the time goes in v1:
time: 111 us; the launch traced here: 110 us
  Pallas kernels  106 us (95%)
  other arithmetic  2 us (2%)
  local copies, waits for them, and re-layouts  1.88 us (2%)
    pallas_call x1, Pallas kernels, local_part(): pl.pallas_call(functools.partial(kernel, n, cores, slots, top), out_shape...  106 us

profile of v1, /device:TPU:99, one launch (start us, length us, event | category | flops | bytes accessed | tf_op | source)
XLA Modules:
  0.0 110.4 jit_solution(3094498882592346417)
XLA Ops:
  0.0 0.7 convert_bitcast_fusion
  0.7 1.3 %select_maximum_fusion.route_ref = f32[16,128]{1,0:T(8,128)} fusion(f32[6,128]{1,0:T(8,128)} %bitcast.5, f32[6,128]{1,0:T(8,128)S(1)} %convert_bitcast_fusion), kind=kLoop, calls=%fused_computation | loop fusion | flops 10240 | bytes 14336 | tf_op jit(solution)/shard_map/concatenate | solution.py:255
  2.0 106.5 %shard_map.73 = bf16[128,2048]{1,0:T(8,128)(2,1)} custom-call(bf16[32,48,2048]{2,1,0:T(8,128)(2,1)} %bitcast.4, bf16[2,2048,1408]{2,1,0:T(8,128)(2,1)} %wg_hbm.1, bf16[2,2048,1408]{2,1,0:T(8,128)(2,1)} %wu_hbm.1, bf16[2,1408,2048]{2,1,0:T(8,128)(2,1)} %wd_hbm.1, f32[16,128]{1,0:T(8,128)} %select_maximum_fusion.route_ref), custom_call_target="tpu_custom_call" | custom-call | tf_op jit(solution)/shard_map/pallas_call | solution.py:261
  108.5 1.9 %copy.9 = bf16[128,2048]{1,0:T(8,128)(2,1)} copy(bf16[128,2048]{1,0:T(8,128)(2,1)} %shard_map.73) | data formatting | bytes 1048576

commit v2 on v0

v2 whole, which is shorter than its diff:
```python
import functools

import jax
import jax.numpy as jnp
from jax import lax
from jax.experimental import pallas as pl
from jax.experimental.pallas import tpu as pltpu
from jax.sharding import PartitionSpec as P

GROUP_AXES = ('eo', 'em', 'ei')
MESH = pl.DeviceIdType.MESH
TILE = 256
DOWN_TILE = 512
ROUTE_ROWS = 8
PAIR = (1, 3)
SINGLE = (2, 0)


def kernel(n, cores, slots, top, x_hbm, wg_hbm, wu_hbm, wd_hbm, slot_hbm, expert_hbm, gate_hbm, out_ref,
           wg, wu, wl, wd, xs, xe, hid, ybuf, recv, part, prec, own, slot_ref, expert_ref, gate_ref, packed, routes,
           gu_sem, wl_sem, wd_sem, x_sem, route_sem, s1, r1, s2, r2, s3, r3):
    experts, model, ff = wg_hbm.shape
    ff_main = wg.shape[2]
    half = ff - ff_main
    rows = 2 * slots
    blocks = 2 * n
    stages = 2 * experts
    tokens = out_ref.shape[0]
    y, x, c = (lax.axis_index(a) for a in GROUP_AXES)
    ring = jnp.where(c == 0, x, y)
    along_y = jnp.where(c == 0, 1, 0)

    def wrap(v):
        return lax.rem(v, n)

    barrier = pltpu.get_barrier_semaphore()
    for oy in range(n):
        for ox in range(n):
            for oc in range(cores):
                if oy or ox or oc:
                    pl.semaphore_signal(barrier, inc=1, device_id_type=MESH, device_id={
                        'eo': wrap(y + oy), 'em': wrap(x + ox), 'ei': lax.rem(c + oc, cores)})

    def x_copy(t, j, step, d):
        if t == 0:
            src = (wrap(y + step) * n + wrap(x + j)) * cores
        else:
            src = (wrap(y + j) * n + wrap(x + step)) * cores + 1
        return pltpu.make_async_copy(x_hbm.at[src], xs.at[d], x_sem.at[d])

    blocks_in_order = [(t, j) for j in range(n) for t in range(2)]

    def pair_copies():
        return [x_copy(t, j, PAIR[h], (t * n + j) * 2 + h) for t, j in blocks_in_order for h in range(2)]

    def single_copies(i):
        return [x_copy(t, j, SINGLE[i], i * blocks + t * n + j) for t, j in blocks_in_order]

    main_tiles = ff_main // TILE
    down_tiles = model // TILE

    def gate_up_copies(e, k):
        if k < main_tiles:
            cols = pl.ds(k * TILE, TILE)
            return [pltpu.make_async_copy(w.at[e, :, cols], v.at[e, :, cols], gu_sem.at[e, k, a])
                    for a, (w, v) in enumerate(((wg_hbm, wg), (wu_hbm, wu)))]
        cols = pl.ds(ff_main, half)
        return [pltpu.make_async_copy(w.at[e, :, cols], wl.at[e, :, pl.ds(a * half, half)], wl_sem.at[e, a])
                for a, w in enumerate((wg_hbm, wu_hbm))]

    def down_copies(e, k):
        cols = pl.ds(k * TILE, TILE)
        return [pltpu.make_async_copy(wd_hbm.at[e, :, cols], wd.at[e, :, cols], wd_sem.at[e, k])]

    loads = [pltpu.make_async_copy(src, dst, route_sem.at[i]) for i, (src, dst) in enumerate(
        ((slot_hbm, slot_ref), (expert_hbm, expert_ref), (gate_hbm, gate_ref)))]
    for cp in loads:
        cp.start()
    for cp in pair_copies():
        cp.start()
    for e in range(experts):
        for k in range(main_tiles + 1):
            for cp in gate_up_copies(e, k):
                cp.start()
        for k in range(down_tiles):
            for cp in down_copies(e, k):
                cp.start()

    for cp in loads:
        cp.wait()
    slot = slot_ref[...]
    packed[...] = jnp.zeros_like(packed)
    packed[0:top] = jnp.where(slot >= 0, expert_ref[...] * slots + slot, -1).astype(jnp.float32)
    packed[ROUTE_ROWS:ROUTE_ROWS + top] = gate_ref[...]

    def ahead(step):
        return {'eo': wrap(y + step * along_y), 'em': wrap(x + step * (1 - along_y)), 'ei': c}

    def route_send(step):
        return pltpu.make_async_remote_copy(
            src_ref=packed, dst_ref=routes.at[step - 1], send_sem=s3.at[step - 1], recv_sem=r3.at[step - 1],
            device_id=ahead(n - step), device_id_type=MESH)

    def arrange_pair():
        for cp in pair_copies():
            cp.wait()
        for k in range(0, model, TILE):
            cols = pl.ds(k, TILE)
            for b in range(blocks):
                first, second = (xs[2 * b + h, :, cols].astype(jnp.float32) for h in range(2))
                for e in range(experts):
                    part_rows = slice(e * slots, (e + 1) * slots)
                    xe[e, pl.ds(b * rows, rows), cols] = jnp.concatenate(
                        [first[part_rows], second[part_rows]], axis=0).astype(jnp.bfloat16)

    def arrange_single(i):
        for b in range(blocks):
            d = i * blocks + b
            pltpu.make_async_copy(x_hbm.at[0], xs.at[d], x_sem.at[d]).wait()
        for k in range(0, model, TILE):
            cols = pl.ds(k, TILE)
            for b in range(0, blocks, 2):
                first, second = (xs[i * blocks + b + h, :, cols].astype(jnp.float32) for h in range(2))
                for e in range(experts):
                    part_rows = slice(e * slots, (e + 1) * slots)
                    xe[e, pl.ds(b * slots, rows), cols] = jnp.concatenate(
                        [first[part_rows], second[part_rows]], axis=0).astype(jnp.bfloat16)

    def gate_up(e, k, count, at):
        dst = pl.ds(at, count)
        lhs = xe[e, 0:count]
        if k < main_tiles:
            cols = pl.ds(k * TILE, TILE)
            g = jnp.dot(lhs, wg[e, :, cols], preferred_element_type=jnp.float32)
            u = jnp.dot(lhs, wu[e, :, cols], preferred_element_type=jnp.float32)
            hid[dst, cols] = (jax.nn.silu(g) * u).astype(jnp.bfloat16)
        else:
            gu = jnp.dot(lhs, wl[e], preferred_element_type=jnp.float32)
            hid[dst, pl.ds(ff_main, half)] = (jax.nn.silu(gu[:, :half]) * gu[:, half:]).astype(jnp.bfloat16)

    def down_pair(s, e, k):
        cols = pl.ds(k, DOWN_TILE)
        out = jnp.dot(hid[...], wd[e, :, cols], preferred_element_type=jnp.float32).astype(jnp.bfloat16)
        ybuf[s, :, :, cols] = out.reshape(blocks, rows, DOWN_TILE)

    def down_single(s, k):
        cols = pl.ds(k, TILE)
        outs = [jnp.dot(hid[pl.ds(e * blocks * slots, blocks * slots)], wd[e, :, cols],
                        preferred_element_type=jnp.float32) for e in range(experts)]
        for b in range(blocks):
            block = jnp.concatenate([v[b * slots:(b + 1) * slots] for v in outs], axis=0)
            ybuf[s, b, :, cols] = block.astype(jnp.bfloat16)

    def row_sends(s):
        out = []
        for j in range(1, n):
            out.append(pltpu.make_async_remote_copy(
                src_ref=ybuf.at[s, j], dst_ref=recv.at[s, x, c], send_sem=s1.at[s, j],
                recv_sem=r1.at[s, x, c], device_id={'eo': y, 'em': wrap(x + j), 'ei': 0}, device_id_type=MESH))
            out.append(pltpu.make_async_remote_copy(
                src_ref=ybuf.at[s, n + j], dst_ref=recv.at[s, y, c], send_sem=s1.at[s, n + j],
                recv_sem=r1.at[s, y, c], device_id={'eo': wrap(y + j), 'em': x, 'ei': 1}, device_id_type=MESH))
        other = 1 - c
        q = jnp.where(c == 0, y, x)
        out.append(pltpu.make_async_remote_copy(
            src_ref=ybuf.at[s, other * n], dst_ref=recv.at[s, q, c], send_sem=s1.at[s, other * n],
            recv_sem=r1.at[s, q, c], device_id={'eo': y, 'em': x, 'ei': other}, device_id_type=MESH))
        return out

    def send_rows(s):
        for cp in row_sends(s):
            cp.start()
        recv[s, ring, c] = ybuf[s, c * n]

    def wait_rows(s):
        def one(q, cc):
            pltpu.make_async_remote_copy(
                src_ref=ybuf.at[s, 0], dst_ref=recv.at[s, q, cc], send_sem=s1.at[s, 0],
                recv_sem=r1.at[s, q, cc], device_id={'eo': y, 'em': x, 'ei': 1 - c},
                device_id_type=MESH).wait_recv()
        one(ring, 1 - c)
        for j in range(1, n):
            for cc in range(cores):
                one(wrap(ring + j), cc)

    def part_send(step):
        return pltpu.make_async_remote_copy(
            src_ref=part.at[step - 1], dst_ref=prec.at[step - 1], send_sem=s2.at[step - 1], recv_sem=r2.at[step - 1],
            device_id=ahead(step), device_id_type=MESH)

    def combine(order, route, store):
        chip = cores * experts
        base = jnp.where(c == 0, y * (n * chip), x * chip)
        jump = jnp.where(c == 0, chip, n * chip)
        row = lax.broadcasted_iota(jnp.int32, (slots, tokens), 0)
        weights, live = [], []
        for _, q, cc, e, _ in order:
            expert = base + q * jump + cc * experts + e
            key = (row + expert * slots).astype(jnp.float32)
            w = jnp.zeros((slots, tokens), jnp.float32)
            for j in range(top):
                w = w + jnp.where(route[j:j + 1, :] == key, route[ROUTE_ROWS + j:ROUTE_ROWS + j + 1, :], 0.0)
            weights.append(w)
            live.append(jnp.max(w, axis=1, keepdims=True) > 0)
        weight = jnp.concatenate(weights, axis=0)
        hi = weight.astype(jnp.bfloat16)
        rest = weight - hi.astype(jnp.float32)
        mid = rest.astype(jnp.bfloat16)
        low = (rest - mid.astype(jnp.float32)).astype(jnp.bfloat16)
        lhs = jnp.concatenate([hi, mid, low], axis=1)
        for k in range(down_tiles):
            cols = pl.ds(k * TILE, TILE)
            got = []
            for (s, q, cc, _, at), keep in zip(order, live):
                block = recv[s, q, cc, :, cols].astype(jnp.float32)
                got.append(jnp.where(keep, block[at * slots:(at + 1) * slots], 0.0))
            got = jnp.concatenate(got, axis=0).astype(jnp.bfloat16)
            p = lax.dot_general(lhs, got, (((0,), (0,)), ((), ())), preferred_element_type=jnp.float32)
            store(cols, (p[2 * tokens:] + p[tokens:2 * tokens]) + p[:tokens])

    def combine_group(step, order):
        def store(cols, value):
            if step:
                part[step - 1, :, cols] = value
            else:
                own[:, cols] = value

        combine(order, routes[step - 1] if step else packed[...], store)
        if step:
            part_send(step).start()

    senders = [(q, cc) for q in range(n) for cc in range(cores)]

    @pl.loop(0, experts)
    def _(s):
        @pl.when(s == 0)
        def _():
            arrange_pair()
            for i in range(2):
                for cp in single_copies(i):
                    cp.start()

        for m in range(experts):
            @pl.when(s == m)
            def _():
                for k in range(main_tiles + 1):
                    for cp in gate_up_copies(m, k):
                        cp.wait()
        for k in range(main_tiles + 1):
            gate_up(s, k, blocks * rows, 0)
        for m in range(experts):
            @pl.when(s == m)
            def _():
                for k in range(down_tiles):
                    for cp in down_copies(m, k):
                        cp.wait()
        for k in range(0, model, DOWN_TILE):
            down_pair(s, s, k)

        @pl.when(s == 0)
        def _():
            pl.semaphore_wait(barrier, n * n * cores - 1)
            for step in range(1, n):
                route_send(step).start()

        send_rows(s)

    @pl.loop(experts, stages)
    def _(s):
        arrange_single(s - experts)
        for e in range(experts):
            for k in range(main_tiles + 1):
                gate_up(e, k, blocks * slots, e * blocks * slots)
        for k in range(0, model, TILE):
            down_single(s, k)
        send_rows(s)

        @pl.when(s == experts)
        def _():
            for step in range(1, n):
                route_send(step).wait_recv()
            for e in range(experts):
                wait_rows(e)
            for h in range(2):
                combine_group(PAIR[h], [(e, q, cc, e, h) for e in range(experts) for q, cc in senders])

    for i in range(2):
        wait_rows(experts + i)
        combine_group(SINGLE[i], [(experts + i, q, cc, e, e) for q, cc in senders for e in range(experts)])
    for step in range(1, n):
        part_send(step).wait_recv()
    for k in range(down_tiles):
        cols = pl.ds(k * TILE, TILE)
        total = own[:, cols]
        for i in range(n - 1):
            total = total + prec[i, :, cols]
        out_ref[:, cols] = total.astype(out_ref.dtype)
    for step in range(1, n):
        part_send(step).wait_send()
        route_send(step).wait_send()

    @pl.loop(0, stages)
    def _(s):
        for cp in row_sends(s):
            cp.wait_send()


def solution(mesh):
    token_spec = P(('dp',) + GROUP_AXES, None)
    weight_spec = P(GROUP_AXES, None, None)
    rows_spec = P('dp', GROUP_AXES, None, None)
    n, cores = mesh.shape['eo'], mesh.shape['ei']
    assert mesh.shape['em'] == n == 4 and cores == 2

    def local_part(x_local, w_gate, w_up, w_down, slot_idx, expert_idx, gate_wt):
        sources, experts, slots, model = x_local.shape
        ff = w_gate.shape[2]
        tokens, top = slot_idx.shape
        ff_main = ff // TILE * TILE
        half = ff - ff_main
        assert 2 * half == TILE and experts == 2
        rows = 2 * slots
        blocks = 2 * n
        stages = 2 * experts
        hbm = pl.BlockSpec(memory_space=pl.ANY)
        vmem = pl.BlockSpec(memory_space=pltpu.VMEM)
        dma = pltpu.SemaphoreType.DMA
        return pl.pallas_call(
            functools.partial(kernel, n, cores, slots, top),
            out_shape=jax.ShapeDtypeStruct((tokens, model), jnp.bfloat16),
            in_specs=[hbm] * 7,
            out_specs=vmem,
            scratch_shapes=[
                pltpu.VMEM((experts, model, ff_main), jnp.bfloat16),
                pltpu.VMEM((experts, model, ff_main), jnp.bfloat16),
                pltpu.VMEM((experts, model, 2 * half), jnp.bfloat16),
                pltpu.VMEM((experts, ff, model), jnp.bfloat16),
                pltpu.VMEM((2 * blocks, experts * slots, model), jnp.bfloat16),
                pltpu.VMEM((experts, blocks * rows, model), jnp.bfloat16),
                pltpu.VMEM((blocks * rows, ff), jnp.bfloat16),
                pltpu.VMEM((stages, blocks, rows, model), jnp.bfloat16),
                pltpu.VMEM((stages, n, cores, rows, model), jnp.bfloat16),
                pltpu.VMEM((n - 1, tokens, model), jnp.float32),
                pltpu.VMEM((n - 1, tokens, model), jnp.float32),
                pltpu.VMEM((tokens, model), jnp.float32),
                pltpu.VMEM((top, tokens), jnp.int32),
                pltpu.VMEM((top, tokens), jnp.int32),
                pltpu.VMEM((top, tokens), jnp.float32),
                pltpu.VMEM((2 * ROUTE_ROWS, tokens), jnp.float32),
                pltpu.VMEM((n - 1, 2 * ROUTE_ROWS, tokens), jnp.float32),
                dma((experts, ff_main // TILE, 2)), dma((experts, 2)), dma((experts, model // TILE)), dma((2 * blocks,)), dma((3,)),
                dma((stages, blocks)), dma((stages, n, cores)), dma((n - 1,)), dma((n - 1,)), dma((n - 1,)), dma((n - 1,)),
            ],
            compiler_params=pltpu.CompilerParams(
                collective_id=0, has_side_effects=True, vmem_limit_bytes=67_000_000),
        )(x_local.reshape(sources, experts * slots, model), w_gate, w_up, w_down, slot_idx.T, expert_idx.T, gate_wt.T)

    return jax.shard_map(local_part, mesh=mesh,
                         in_specs=(rows_spec, weight_spec, weight_spec, weight_spec, token_spec, token_spec, token_spec),
                         out_specs=token_spec, check_vma=False)
```

time: 163 us -> 87.2 us (0.53)
  the two profiles are of different devices: /device:TPU:103 before, /device:TPU:98 now
where the time goes in v2:
time: 87.2 us; the launch traced here: 87 us
  Pallas kernels  85.2 us (98%)
  local copies, waits for them, and re-layouts  1.88 us (2%)
    pallas_call x1, Pallas kernels, local_part(): pl.pallas_call(functools.partial(kernel, n, cores, slots, top), out_shape...  85.2 us
    unnamed x1, local copies, waits for them, and re-layouts  1.88 us

profile of v2, /device:TPU:98, one launch (start us, length us, event | category | flops | bytes accessed | tf_op | source)
XLA Modules:
  0.0 87.0 jit_solution(7556145744388231836)
XLA Ops:
  0.0 85.2 %shard_map.73 = bf16[128,2048]{1,0:T(8,128)(2,1)} custom-call(bf16[32,48,2048]{2,1,0:T(8,128)(2,1)} %bitcast.4, bf16[2,2048,1408]{2,1,0:T(8,128)(2,1)} %wg_hbm.1, bf16[2,2048,1408]{2,1,0:T(8,128)(2,1)} %wu_hbm.1, bf16[2,1408,2048]{2,1,0:T(8,128)(2,1)} %wd_hbm.1, s32[6,128]{1,0:T(8,128)} %bitcast.5, s32[6,128]{1,0:T(8,128)} %bitcast.6, f32[6,128]{1,0:T(8,128)} %bitcast.7), custom_call_target="tpu_custom_call" | custom-call | tf_op jit(solution)/shard_map/pallas_call | solution.py:328
  85.2 1.9 %copy.9 = bf16[128,2048]{1,0:T(8,128)(2,1)} copy(bf16[128,2048]{1,0:T(8,128)(2,1)} %shard_map.73) | data formatting | bytes 1048576

commit v3 on v2

v3 whole, which is shorter than its diff:
```python
import functools

import jax
import jax.numpy as jnp
from jax import lax
from jax.experimental import pallas as pl
from jax.experimental.pallas import tpu as pltpu
from jax.sharding import PartitionSpec as P

GROUP_AXES = ('eo', 'em', 'ei')
MESH = pl.DeviceIdType.MESH
TILE = 256
DOWN_TILE = 512
ROUTE_ROWS = 8
PAIR = (2, 1)
SINGLE = (3, 0)
ORDER = ((0, 1), (1, 1), (0, 3), (1, 3), (0, 2), (1, 2), (0, 0), (1, 0))


def kernel(n, cores, slots, top, x_hbm, wg_hbm, wu_hbm, wd_hbm, slot_hbm, expert_hbm, gate_hbm, out_ref,
           wg, wu, wl, wd, xs, xe, hid, ybuf, recv, part, mid_in, prec, slot_ref, expert_ref, gate_ref, packed, routes,
           gu_sem, wl_sem, wd_sem, x_sem, route_sem, s1, r1, s2, r2, s3, r3, s4, r4):
    experts, model, ff = wg_hbm.shape
    ff_main = wg.shape[2]
    half = ff - ff_main
    rows = 2 * slots
    blocks = 2 * n
    part_blocks = blocks // 2
    stages = 2 * experts
    tokens = out_ref.shape[0]
    y, x, c = (lax.axis_index(a) for a in GROUP_AXES)
    ring = jnp.where(c == 0, x, y)
    along_y = jnp.where(c == 0, 1, 0)

    def wrap(v):
        return lax.rem(v, n)

    def ahead(step):
        return {'eo': wrap(y + step * along_y), 'em': wrap(x + step * (1 - along_y)), 'ei': c}

    def x_copy(t, j, step, d):
        if t == 0:
            src = (wrap(y + step) * n + wrap(x + j)) * cores
        else:
            src = (wrap(y + j) * n + wrap(x + step)) * cores + 1
        return pltpu.make_async_copy(x_hbm.at[src], xs.at[d], x_sem.at[d])

    def pair_copies():
        return [x_copy(t, j, PAIR[h], 2 * p + h) for p, (t, j) in enumerate(ORDER) for h in range(2)]

    def single_copies(i):
        return [x_copy(t, j, SINGLE[i], i * blocks + p) for p, (t, j) in enumerate(ORDER)]

    main_tiles = ff_main // TILE
    down_tiles = model // TILE

    def gate_up_copies(e):
        out = []
        for a, (w, v) in enumerate(((wg_hbm, wg), (wu_hbm, wu))):
            out.append(pltpu.make_async_copy(w.at[e, :, pl.ds(0, ff_main)], v.at[e], gu_sem.at[e, a]))
            out.append(pltpu.make_async_copy(
                w.at[e, :, pl.ds(ff_main, half)], wl.at[e, :, pl.ds(a * half, half)], wl_sem.at[e, a]))
        return out

    def down_copy(e):
        return pltpu.make_async_copy(wd_hbm.at[e], wd.at[e], wd_sem.at[e])

    loads = [pltpu.make_async_copy(src, dst, route_sem.at[i]) for i, (src, dst) in enumerate(
        ((slot_hbm, slot_ref), (expert_hbm, expert_ref), (gate_hbm, gate_ref)))]
    for cp in loads:
        cp.start()
    for cp in pair_copies():
        cp.start()
    for e in range(experts):
        for cp in gate_up_copies(e):
            cp.start()
        down_copy(e).start()

    barrier = pltpu.get_barrier_semaphore()
    writers = [{'eo': y, 'em': x, 'ei': 1 - c}]
    for j in range(1, n):
        writers += [{'eo': wrap(y + j * (1 - along_y)), 'em': wrap(x + j * along_y), 'ei': cc} for cc in range(cores)]
        writers.append(ahead(j))
    for device in writers:
        pl.semaphore_signal(barrier, inc=1, device_id=device, device_id_type=MESH)

    for cp in loads:
        cp.wait()
    slot = slot_ref[...]
    packed[...] = jnp.zeros_like(packed)
    packed[0:top] = jnp.where(slot >= 0, expert_ref[...] * slots + slot, -1).astype(jnp.float32)
    packed[ROUTE_ROWS:ROUTE_ROWS + top] = gate_ref[...]

    def route_send(step):
        return pltpu.make_async_remote_copy(
            src_ref=packed, dst_ref=routes.at[step - 1], send_sem=s3.at[step - 1], recv_sem=r3.at[step - 1],
            device_id=ahead(n - step), device_id_type=MESH)

    def wait_x(first, count):
        for b in range(count):
            pltpu.make_async_copy(x_hbm.at[0], xs.at[first + b], x_sem.at[first + b]).wait()

    def arrange_pair(p):
        wait_x(p * blocks, blocks)
        for k in range(0, model, TILE):
            cols = pl.ds(k, TILE)
            for b in range(part_blocks):
                first, second = (xs[p * blocks + 2 * b + h, :, cols].astype(jnp.float32) for h in range(2))
                for e in range(experts):
                    part_rows = slice(e * slots, (e + 1) * slots)
                    xe[e, p, pl.ds(b * rows, rows), cols] = jnp.concatenate(
                        [first[part_rows], second[part_rows]], axis=0).astype(jnp.bfloat16)

    def arrange_single(i):
        wait_x(i * blocks, blocks)
        for k in range(0, model, TILE):
            cols = pl.ds(k, TILE)
            for b in range(0, blocks, 2):
                first, second = (xs[i * blocks + b + h, :, cols].astype(jnp.float32) for h in range(2))
                for e in range(experts):
                    part_rows = slice(e * slots, (e + 1) * slots)
                    xe[e, 0, pl.ds(b * slots, rows), cols] = jnp.concatenate(
                        [first[part_rows], second[part_rows]], axis=0).astype(jnp.bfloat16)

    def gate_up(e, p, k, at):
        dst = pl.ds(at, blocks * slots)
        lhs = xe[e, p]
        if k < main_tiles:
            cols = pl.ds(k * TILE, TILE)
            g = jnp.dot(lhs, wg[e, :, cols], preferred_element_type=jnp.float32)
            u = jnp.dot(lhs, wu[e, :, cols], preferred_element_type=jnp.float32)
            hid[dst, cols] = (jax.nn.silu(g) * u).astype(jnp.bfloat16)
        else:
            gu = jnp.dot(lhs, wl[e], preferred_element_type=jnp.float32)
            hid[dst, pl.ds(ff_main, half)] = (jax.nn.silu(gu[:, :half]) * gu[:, half:]).astype(jnp.bfloat16)

    def down_pair(e, p, k):
        cols = pl.ds(k, DOWN_TILE)
        out = jnp.dot(hid[0:blocks * slots], wd[e, :, cols], preferred_element_type=jnp.float32).astype(jnp.bfloat16)
        ybuf[e, pl.ds(p * part_blocks, part_blocks), :, cols] = out.reshape(part_blocks, rows, DOWN_TILE)

    def down_single(s, k):
        cols = pl.ds(k, TILE)
        outs = [jnp.dot(hid[pl.ds(e * blocks * slots, blocks * slots)], wd[e, :, cols],
                        preferred_element_type=jnp.float32) for e in range(experts)]
        for b in range(blocks):
            block = jnp.concatenate([v[b * slots:(b + 1) * slots] for v in outs], axis=0)
            ybuf[s, b, :, cols] = block.astype(jnp.bfloat16)

    def row_sends(s, where):
        out = []
        for p in where:
            t, j = ORDER[p]
            if j and t == 0:
                out.append(pltpu.make_async_remote_copy(
                    src_ref=ybuf.at[s, p], dst_ref=recv.at[s, x, c], send_sem=s1.at[s, p],
                    recv_sem=r1.at[s, x, c], device_id={'eo': y, 'em': wrap(x + j), 'ei': 0}, device_id_type=MESH))
            elif j:
                out.append(pltpu.make_async_remote_copy(
                    src_ref=ybuf.at[s, p], dst_ref=recv.at[s, y, c], send_sem=s1.at[s, p],
                    recv_sem=r1.at[s, y, c], device_id={'eo': wrap(y + j), 'em': x, 'ei': 1}, device_id_type=MESH))
        if blocks - 1 in where:
            p = blocks - 1 - c
            q = jnp.where(c == 0, y, x)
            out.append(pltpu.make_async_remote_copy(
                src_ref=ybuf.at[s, p], dst_ref=recv.at[s, q, c], send_sem=s1.at[s, p],
                recv_sem=r1.at[s, q, c], device_id={'eo': y, 'em': x, 'ei': 1 - c}, device_id_type=MESH))
        return out

    near, far = range(part_blocks), range(part_blocks, blocks)

    def send_rows(s, where):
        for cp in row_sends(s, where):
            cp.start()
        if blocks - 1 in where:
            recv[s, ring, c] = ybuf[s, blocks - 2 + c]

    def wait_rows(s):
        def one(q, cc):
            pltpu.make_async_remote_copy(
                src_ref=ybuf.at[s, 0], dst_ref=recv.at[s, q, cc], send_sem=s1.at[s, 0],
                recv_sem=r1.at[s, q, cc], device_id={'eo': y, 'em': x, 'ei': 1 - c},
                device_id_type=MESH).wait_recv()
        one(ring, 1 - c)
        for j in range(1, n):
            for cc in range(cores):
                one(wrap(ring + j), cc)

    ways = (1, n - 1)

    def middle_send(h):
        return pltpu.make_async_remote_copy(
            src_ref=part.at[2, h], dst_ref=mid_in.at[h], send_sem=s4.at[h], recv_sem=r4.at[h],
            device_id=ahead(ways[h]), device_id_type=MESH)

    def part_send(way, h):
        return pltpu.make_async_remote_copy(
            src_ref=part.at[ways[way], h], dst_ref=prec.at[way, h], send_sem=s2.at[way, h], recv_sem=r2.at[way, h],
            device_id=ahead(ways[way]), device_id_type=MESH)

    def finish_part(way):
        middle_send(way).wait_recv()
        part[ways[way], way] = part[ways[way], way] + mid_in[way]
        part_send(way, way).start()

    def combine(step, order):
        route = routes[step - 1] if step else packed[...]
        chip = cores * experts
        base = jnp.where(c == 0, y * (n * chip), x * chip)
        jump = jnp.where(c == 0, chip, n * chip)
        row = lax.broadcasted_iota(jnp.int32, (slots, tokens), 0)
        weights, live = [], []
        for _, q, cc, e, _ in order:
            expert = base + q * jump + cc * experts + e
            key = (row + expert * slots).astype(jnp.float32)
            w = jnp.zeros((slots, tokens), jnp.float32)
            for j in range(top):
                w = w + jnp.where(route[j:j + 1, :] == key, route[ROUTE_ROWS + j:ROUTE_ROWS + j + 1, :], 0.0)
            weights.append(w)
            live.append(jnp.max(w, axis=1, keepdims=True) > 0)
        weight = jnp.concatenate(weights, axis=0)
        hi = weight.astype(jnp.bfloat16)
        rest = weight - hi.astype(jnp.float32)
        mid = rest.astype(jnp.bfloat16)
        low = (rest - mid.astype(jnp.float32)).astype(jnp.bfloat16)
        lhs = jnp.concatenate([hi, mid, low], axis=1)
        for k in range(down_tiles):
            cols = pl.ds(k * TILE, TILE)
            got = []
            for (s, q, cc, _, at), keep in zip(order, live):
                block = recv[s, q, cc, :, cols].astype(jnp.float32)
                got.append(jnp.where(keep, block[at * slots:(at + 1) * slots], 0.0))
            got = jnp.concatenate(got, axis=0).astype(jnp.bfloat16)
            p = lax.dot_general(lhs, got, (((0,), (0,)), ((), ())), preferred_element_type=jnp.float32)
            part[step, k // (down_tiles // 2), :, pl.ds(k % (down_tiles // 2) * TILE, TILE)] = (
                (p[2 * tokens:] + p[tokens:2 * tokens]) + p[:tokens])

    senders = [(q, cc) for q in range(n) for cc in range(cores)]

    @pl.loop(0, 2 * experts)
    def _(u):
        e, p = u // 2, lax.rem(u, 2)

        @pl.when(u < 2)
        def _():
            arrange_pair(p)

        @pl.when(u == 1)
        def _():
            for i in range(2):
                for cp in single_copies(i):
                    cp.start()

        for m in range(experts):
            @pl.when(u == 2 * m)
            def _():
                for cp in gate_up_copies(m):
                    cp.wait()
        for k in range(main_tiles + 1):
            gate_up(e, p, k, 0)
        for m in range(experts):
            @pl.when(u == 2 * m)
            def _():
                down_copy(m).wait()
        for k in range(0, model, DOWN_TILE):
            down_pair(e, p, k)

        @pl.when(u == 0)
        def _():
            pl.semaphore_wait(barrier, len(writers))
            for step in range(1, n):
                route_send(step).start()

        @pl.when(p == 0)
        def _():
            send_rows(e, near)

        @pl.when(p == 1)
        def _():
            send_rows(e, far)

    @pl.loop(experts, stages)
    def _(s):
        arrange_single(s - experts)
        for e in range(experts):
            for k in range(main_tiles + 1):
                gate_up(e, 0, k, e * blocks * slots)
        for k in range(0, model, TILE):
            down_single(s, k)
        send_rows(s, range(blocks))

        @pl.when(s == experts)
        def _():
            for step in range(1, n):
                route_send(step).wait_recv()
            for e in range(experts):
                wait_rows(e)
            for h in range(2):
                combine(PAIR[h], [(e, q, cc, e, h) for e in range(experts) for q, cc in senders])
                if h == 0:
                    for way in range(2):
                        middle_send(way).start()
                else:
                    part_send(0, 1).start()

    finish_part(0)
    for i in range(2):
        wait_rows(experts + i)
        combine(SINGLE[i], [(experts + i, q, cc, e, e) for q, cc in senders for e in range(experts)])
        if i == 0:
            part_send(1, 0).start()
            finish_part(1)
    for h in range(2):
        for way in range(2):
            part_send(way, h).wait_recv()
        for k in range(0, model // 2, TILE):
            cols = pl.ds(k, TILE)
            total = part[0, h, :, cols] + prec[0, h, :, cols] + prec[1, h, :, cols]
            out_ref[:, pl.ds(h * (model // 2) + k, TILE)] = total.astype(out_ref.dtype)
    for way in range(2):
        middle_send(way).wait_send()
        for h in range(2):
            part_send(way, h).wait_send()
    for step in range(1, n):
        route_send(step).wait_send()

    @pl.loop(0, stages)
    def _(s):
        for cp in row_sends(s, range(blocks)):
            cp.wait_send()


def solution(mesh):
    token_spec = P(('dp',) + GROUP_AXES, None)
    weight_spec = P(GROUP_AXES, None, None)
    rows_spec = P('dp', GROUP_AXES, None, None)
    n, cores = mesh.shape['eo'], mesh.shape['ei']
    assert mesh.shape['em'] == n == 4 and cores == 2

    def local_part(x_local, w_gate, w_up, w_down, slot_idx, expert_idx, gate_wt):
        sources, experts, slots, model = x_local.shape
        ff = w_gate.shape[2]
        tokens, top = slot_idx.shape
        ff_main = ff // TILE * TILE
        half = ff - ff_main
        assert 2 * half == TILE and experts == 2
        rows = 2 * slots
        blocks = 2 * n
        stages = 2 * experts
        hbm = pl.BlockSpec(memory_space=pl.ANY)
        vmem = pl.BlockSpec(memory_space=pltpu.VMEM)
        dma = pltpu.SemaphoreType.DMA
        return pl.pallas_call(
            functools.partial(kernel, n, cores, slots, top),
            out_shape=jax.ShapeDtypeStruct((tokens, model), jnp.bfloat16),
            in_specs=[hbm] * 7,
            out_specs=vmem,
            scratch_shapes=[
                pltpu.VMEM((experts, model, ff_main), jnp.bfloat16),
                pltpu.VMEM((experts, model, ff_main), jnp.bfloat16),
                pltpu.VMEM((experts, model, 2 * half), jnp.bfloat16),
                pltpu.VMEM((experts, ff, model), jnp.bfloat16),
                pltpu.VMEM((2 * blocks, experts * slots, model), jnp.bfloat16),
                pltpu.VMEM((experts, 2, blocks * slots, model), jnp.bfloat16),
                pltpu.VMEM((experts * blocks * slots, ff), jnp.bfloat16),
                pltpu.VMEM((stages, blocks, rows, model), jnp.bfloat16),
                pltpu.VMEM((stages, n, cores, rows, model), jnp.bfloat16),
                pltpu.VMEM((n, 2, tokens, model // 2), jnp.float32),
                pltpu.VMEM((2, tokens, model // 2), jnp.float32),
                pltpu.VMEM((2, 2, tokens, model // 2), jnp.float32),
                pltpu.VMEM((top, tokens), jnp.int32),
                pltpu.VMEM((top, tokens), jnp.int32),
                pltpu.VMEM((top, tokens), jnp.float32),
                pltpu.VMEM((2 * ROUTE_ROWS, tokens), jnp.float32),
                pltpu.VMEM((n - 1, 2 * ROUTE_ROWS, tokens), jnp.float32),
                dma((experts, 2)), dma((experts, 2)), dma((experts,)), dma((2 * blocks,)), dma((3,)),
                dma((stages, blocks)), dma((stages, n, cores)), dma((2, 2)), dma((2, 2)), dma((n - 1,)), dma((n - 1,)), dma((2,)), dma((2,)),
            ],
            compiler_params=pltpu.CompilerParams(
                collective_id=0, has_side_effects=True, vmem_limit_bytes=67_000_000),
        )(x_local.reshape(sources, experts * slots, model), w_gate, w_up, w_down, slot_idx.T, expert_idx.T, gate_wt.T)

    return jax.shard_map(local_part, mesh=mesh,
                         in_specs=(rows_spec, weight_spec, weight_spec, weight_spec, token_spec, token_spec, token_spec),
                         out_specs=token_spec, check_vma=False)
```

time: 87.2 us -> 77.1 us (0.88)
  Pallas kernels: 85.2 us -> 75.1 us
    pallas_call x1, Pallas kernels: 85.2 us -> 75.1 us  [local_part(): pl.pallas_call(functools.partial(kernel, n, cores, slots, top), out_shape...]
where the time goes in v3:
time: 77.1 us; the launch traced here: 77 us
  Pallas kernels  75.1 us (97%)
  local copies, waits for them, and re-layouts  1.88 us (2%)
    pallas_call x1, Pallas kernels, local_part(): pl.pallas_call(functools.partial(kernel, n, cores, slots, top), out_shape...  75.1 us
    unnamed x1, local copies, waits for them, and re-layouts  1.88 us

profile of v3, /device:TPU:98, one launch (start us, length us, event | category | flops | bytes accessed | tf_op | source)
XLA Modules:
  0.0 77.0 jit_solution(8281063933697504536)
XLA Ops:
  0.0 75.1 %shard_map.73 = bf16[128,2048]{1,0:T(8,128)(2,1)} custom-call(bf16[32,48,2048]{2,1,0:T(8,128)(2,1)} %bitcast.4, bf16[2,2048,1408]{2,1,0:T(8,128)(2,1)} %wg_hbm.1, bf16[2,2048,1408]{2,1,0:T(8,128)(2,1)} %wu_hbm.1, bf16[2,1408,2048]{2,1,0:T(8,128)(2,1)} %wd_hbm.1, s32[6,128]{1,0:T(8,128)} %bitcast.5, s32[6,128]{1,0:T(8,128)} %bitcast.6, f32[6,128]{1,0:T(8,128)} %bitcast.7), custom_call_target="tpu_custom_call" | custom-call | tf_op jit(solution)/shard_map/pallas_call | solution.py:353
  75.1 1.9 %copy.9 = bf16[128,2048]{1,0:T(8,128)(2,1)} copy(bf16[128,2048]{1,0:T(8,128)(2,1)} %shard_map.73) | data formatting | bytes 1048576

commit v4 on v3

--- a/solution.py
+++ b/solution.py
@@ -14,7 +14,7 @@
 ROUTE_ROWS = 8
 PAIR = (2, 1)
 SINGLE = (3, 0)
-ORDER = ((0, 1), (1, 1), (0, 3), (1, 3), (0, 2), (1, 2), (0, 0), (1, 0))
+ORDER = ((0, 2), (1, 2), (0, 1), (1, 1), (0, 3), (1, 3), (0, 0), (1, 0))
 
 
 def kernel(n, cores, slots, top, x_hbm, wg_hbm, wu_hbm, wd_hbm, slot_hbm, expert_hbm, gate_hbm, out_ref,

time: 77.1 us -> 76.5 us (level)
  no operation moved by 1% of the time
where the time goes in v4:
time: 76.5 us; the launch traced here: 76.4 us
  Pallas kernels  74.5 us (97%)
  local copies, waits for them, and re-layouts  1.88 us (2%)
    pallas_call x1, Pallas kernels, local_part(): pl.pallas_call(functools.partial(kernel, n, cores, slots, top), out_shape...  74.5 us
    unnamed x1, local copies, waits for them, and re-layouts  1.88 us

profile of v4, /device:TPU:98, one launch (start us, length us, event | category | flops | bytes accessed | tf_op | source)
XLA Modules:
  0.0 76.4 jit_solution(16276122846204838228)
XLA Ops:
  0.0 74.5 %shard_map.73 = bf16[128,2048]{1,0:T(8,128)(2,1)} custom-call(bf16[32,48,2048]{2,1,0:T(8,128)(2,1)} %bitcast.4, bf16[2,2048,1408]{2,1,0:T(8,128)(2,1)} %wg_hbm.1, bf16[2,2048,1408]{2,1,0:T(8,128)(2,1)} %wu_hbm.1, bf16[2,1408,2048]{2,1,0:T(8,128)(2,1)} %wd_hbm.1, s32[6,128]{1,0:T(8,128)} %bitcast.5, s32[6,128]{1,0:T(8,128)} %bitcast.6, f32[6,128]{1,0:T(8,128)} %bitcast.7), custom_call_target="tpu_custom_call" | custom-call | tf_op jit(solution)/shard_map/pallas_call | solution.py:353
  74.5 1.9 %copy.9 = bf16[128,2048]{1,0:T(8,128)(2,1)} copy(bf16[128,2048]{1,0:T(8,128)(2,1)} %shard_map.73) | data formatting | bytes 1048576
